TPU v7x, 256 devices: a whole 4x4x8 slice. The times are simulated.
256 devices in a mesh: batch: 16 (over z_hi, y), ctx: 16 (over z_lo, x, core).
Axes of the slice: x: 4, y: 4, z: 8 (z_hi: 4, z_lo: 2; z = z_hi * 2 + z_lo), core: 2. Of those that a mesh axis runs over, the one named last changes fastest.
Arguments:
- asked_for: bfloat16 [32, 4096, 16, 128], P('batch', 'ctx'), may hold values from -6 to 6
- offered: bfloat16 [32, 4096, 16, 128], P('batch', 'ctx'), may hold values from -6 to 6
- contents: bfloat16 [32, 4096, 16, 128], P('batch', 'ctx'), may hold values from -6 to 6
- gate_rows: bfloat16 [32, 4096, 16, 128], P('batch', 'ctx'), may hold values from -6 to 6
- out_weight: bfloat16 [2048, 2048], P('batch'), may hold values from -0.125 to 0.125
Outputs:
- block_out: bfloat16 [32, 4096, 2048], P('batch', 'ctx')
All inputs are finite; a program needn't handle non-finite values.
Results may differ from a plain program's by a relative error of at most 0.006.
Values may be sent and summed in bfloat16 or wider, within the bound.
A program may use at most 128 MiB of HBM per device.

v0:
```python
import jax
import jax.numpy as jnp
from jax import lax
from jax.sharding import Mesh
from jax.sharding import PartitionSpec as P

BATCH = ("batch_0", "batch_1")


def laid_out(pieces, dim):
    pieces = jnp.moveaxis(pieces, 0, dim)
    dims = pieces.shape
    return pieces.reshape(*dims[:dim], dims[dim] * dims[dim + 1], *dims[dim + 2 :])


def gather_in_order(shard, axes, turns):
    pieces = shard
    for k in turns:
        pieces = lax.all_gather(pieces, axes[k])
    done = turns[::-1]
    back = [done.index(k) for k in range(len(axes))]
    pieces = pieces.transpose(*back, *range(len(axes), pieces.ndim))
    return pieces.reshape(-1, *shard.shape)


def whole_of(shard, axes, turns, dim):
    return laid_out(gather_in_order(shard, axes, turns), dim)


def to_features(values):
    wide = values.astype(jnp.float32)
    return jnp.where(wide > 0.0, wide + 1.0, jnp.exp(jnp.minimum(wide, 0.0))).astype(jnp.bfloat16)


def close_heads(read, gate_rows, count):
    result = read * count**0.5
    result = result * jax.nn.sigmoid(gate_rows.astype(jnp.float32))
    return result.astype(jnp.bfloat16)


def ask_state(features, state, mass):
    top = jnp.einsum(
        "bthd,bhde->bthe", features, state.astype(jnp.bfloat16), preferred_element_type=jnp.float32
    )
    bottom = jnp.einsum("bthd,bhd->bth", features.astype(jnp.float32), mass)
    return top / (bottom + 0.001)[..., None]


def local(asked_for, offered, contents, gate_rows, out_weight):
    query_feature, key_feature = (to_features(asked_for), to_features(offered))
    count = asked_for.shape[1] * lax.axis_size("ctx")
    part_state = jnp.einsum(
        "bthd,bthe->bhde", key_feature, contents, preferred_element_type=jnp.float32
    )
    part_mass = jnp.sum(key_feature.astype(jnp.float32), axis=1)
    state, mass = lax.psum((part_state, part_mass), "ctx")
    read = ask_state(query_feature, state / count, mass / count)
    mixed = close_heads(read, gate_rows, count)
    mixed = mixed.reshape(mixed.shape[0], mixed.shape[1], -1)
    return jnp.einsum(
        "btw,wv->btv",
        mixed,
        whole_of(out_weight, BATCH, (0, 1), 0),
        preferred_element_type=jnp.float32,
    ).astype(jnp.bfloat16)


def solution(mesh):
    finer = Mesh(mesh.devices.reshape(4, 4, mesh.shape["ctx"]), ("batch_0", "batch_1", "ctx"))
    in_specs = (
        P(BATCH, "ctx", None, None),
        P(BATCH, "ctx", None, None),
        P(BATCH, "ctx", None, None),
        P(BATCH, "ctx", None, None),
        P(BATCH, None),
    )
    out_specs = P(BATCH, "ctx", None)
    return jax.shard_map(local, mesh=finer, in_specs=in_specs, out_specs=out_specs, check_vma=False)
```

profile of v0, /device:TPU:1, one launch (start us, length us, event | category | flops | bytes accessed | tf_op | source)
XLA Modules:
  0.0 203.2 jit_solution(10561103089615189682)
XLA Ops:
  7.4 0.0 copy-start
  7.4 0.0 all-gather.5.cloned.1.call-start
  7.4 0.7 all-gather.5.cloned.1.call-update
  8.1 0.0 all-reduce.2.cloned.1.call-start
  8.1 4.3 %copy.17 = bf16[2,256,16,128]{1,3,2,0:T(8,128)(2,1)} copy(bf16[2,256,16,128]{3,2,1,0:T(8,128)(2,1)} %param.6) | data formatting | bytes 4194304 | tf_op args[1]
  12.4 0.0 copy-done
  12.4 4.4 %fusion.9 = f32[2,16,128,128]{3,2,1,0:T(8,128)} fusion(bf16[2,256,16,128]{3,2,1,0:T(8,128)(2,1)S(1)} %copy-done, bf16[2,256,16,128]{1,3,2,0:T(8,128)(2,1)} %copy.17), kind=kOutput, calls=%fused_computation.18 | convolution fusion | flops 274726912 | bytes 6291456 | tf_op jit(solution)/shard_map/bthd,bthe->bhde/dot_general | solution.py:52
  16.8 0.0 all-reduce.2.cloned.1.call-update
  16.9 0.0 all-gather.7.cloned.1.call-start
  16.9 47.8 %all-gather.5.cloned.1.call-done = bf16[512,2048]{1,0:T(8,128)(2,1)} async-done(((bf16[128,2048]{1,0:T(8,128)(2,1)}), bf16[512,2048]{1,0:T(8,128)(2,1)}) %all-gather.5.cloned.1.call-update) | async-done | bytes 2097168 | tf_op jit(solution)/shard_map/all_gather | solution.py:19
  64.7 0.0 all-gather.7.cloned.1.call-update
  64.7 4.3 %copy.19 = bf16[2,256,16,128]{1,3,2,0:T(8,128)(2,1)} copy(bf16[2,256,16,128]{3,2,1,0:T(8,128)(2,1)} %param.5) | data formatting | bytes 4194304 | tf_op args[0]
  69.0 4.3 %copy.22 = bf16[2,256,16,128]{1,3,2,0:T(8,128)(2,1)} copy(bf16[2,256,16,128]{3,2,1,0:T(8,128)(2,1)} %param.8) | data formatting | bytes 4194304 | tf_op args[3]
  73.3 2.8 %convert_reduce_fusion = f32[2,16,128]{2,1,0:T(8,128)S(1)} fusion(bf16[2,256,16,128]{1,3,2,0:T(8,128)(2,1)} %copy.17), kind=kLoop, calls=%fused_computation.16 | loop fusion | flops 8384512 | bytes 2113536 | tf_op jit(solution)/shard_map/reduce_sum | solution.py:55
  76.1 54.0 %psum.15 = f32[2,16,128]{2,1,0:T(8,128)S(1)} all-reduce(f32[2,16,128]{2,1,0:T(8,128)S(1)} %convert_reduce_fusion), channel_id=1, replica_groups=mesh['batch_0'=4,'batch_1'=4,'ctx'=16] {'ctx'}, use_global_device_ids=true, to_apply=%region_2.3 | all-reduce | flops 4096 | bytes 32768 | tf_op jit(solution)/shard_map/psum | solution.py:56
  130.1 2.8 %fusion.13 = f32[2,16,1,256]{3,2,1,0:T(1,128)S(1)} fusion(f32[2,16,128,1]{2,3,1,0:T(1,128)S(1)} %bitcast.31, bf16[2,256,16,128]{1,3,2,0:T(8,128)(2,1)} %copy.19), kind=kOutput, calls=%fused_computation.22 | convolution fusion | flops 8388608 | bytes 2146304 | tf_op jit(solution)/shard_map/bthd,bhd->bth/dot_general | solution.py:45
  132.8 38.8 %all-reduce.2.cloned.1.call-done = f32[2,16,128,128]{3,2,1,0:T(8,128)} async-done(((f32[2,16,128,128]{3,2,1,0:T(8,128)}), f32[2,16,128,128]{3,2,1,0:T(8,128)}) %all-reduce.2.cloned.1.call-update) | async-done | bytes 2097168 | tf_op jit(solution)/shard_map/psum | solution.py:56
  171.6 6.6 %fusion.8 = bf16[2,256,16,128]{1,3,2,0:T(8,128)(2,1)} fusion(bf16[2,256,16,128]{1,3,2,0:T(8,128)(2,1)} %copy.22, f32[2,256,16]{1,2,0:T(8,128)S(1)} %fusion.16, f32[2,16,128,128]{3,2,1,0:T(8,128)} %all-reduce.2.cloned.1.call-done, bf16[2,256,16,128]{1,3,2,0:T(8,128)(2,1)} %copy.19), kind=kOutput, calls=%fused_computation.15 | convolution fusion | flops 284164096 | bytes 8421376 | tf_op jit(solution)/shard_map/bthd,bhde->bthe/dot_general | solution.py:42
  178.2 0.0 all-gather.7.cloned.1.call-done
  178.2 0.0 copy-start.1
  178.2 8.4 %copy.23 = bf16[4,4,128,2048]{3,2,1,0:T(8,128)(2,1)} copy(bf16[4,4,128,2048]{3,2,0,1:T(8,128)(2,1)} %bitcast.28) | data formatting | bytes 16777216 | tf_op jit(solution)/shard_map/transpose | solution.py:22
  186.6 0.0 copy-done.1
  186.6 9.1 %convolution_convert_fusion = bf16[2,256,2048]{2,1,0:T(8,128)(2,1)} fusion(bf16[2,256,2048]{1,2,0:T(8,128)(2,1)S(1)} %bitcast.32, bf16[2048,2048,1]{1,0,2:T(8,128)(2,1)} %bitcast.29), kind=kOutput, calls=%fused_computation.17 | convolution fusion | flops 4296015872 | bytes 12582912 | tf_op jit(solution)/shard_map/btw,wv->btv/dot_general | solution.py:60
  (2 shorter events, 0.0 us)
Async XLA Ops:
  7.4 5.1 %copy-start = (bf16[2,256,16,128]{3,2,1,0:T(8,128)(2,1)S(1)}, bf16[2,256,16,128]{3,2,1,0:T(8,128)(2,1)}, u32[]{:S(2)}) copy-start(bf16[2,256,16,128]{3,2,1,0:T(8,128)(2,1)} %param.7) | copy-start | bytes 6291460
  7.4 57.3 %all-gather.5.cloned.1.call-start = ((), (), s32[]{:S(2)}) async-start(), calls=%async_computation.1 | async-start | bytes 2621440 | tf_op jit(solution)/shard_map/all_gather | solution.py:19
  8.1 163.6 %all-reduce.2.cloned.1.call-start = ((), (), s32[]{:S(2)}) async-start(), calls=%async_computation | async-start | bytes 4194304 | tf_op jit(solution)/shard_map/psum | solution.py:56
  16.9 161.4 %all-gather.7.cloned.1.call-start = ((), (), s32[]{:S(2)}) async-start(), calls=%async_computation.2 | async-start | bytes 10485760 | tf_op jit(solution)/shard_map/all_gather | solution.py:19
  178.2 8.4 %copy-start.1 = (bf16[2,256,16,128]{1,3,2,0:T(8,128)(2,1)S(1)}, bf16[2,256,16,128]{1,3,2,0:T(8,128)(2,1)}, u32[]{:S(2)}) copy-start(bf16[2,256,16,128]{1,3,2,0:T(8,128)(2,1)} %fusion.8) | copy-start | bytes 6291460
Sparse Core Ops, SparseCore 0:
  10.0 54.6 all-gather.4
  66.5 85.6 all-gather.6
Sparse Core Ops, SparseCore 1:
  16.9 154.7 all-reduce.1
where the time goes:
time: 204 us; the launch traced here: 203 us
  waiting for transfers between devices  87.3 us (43%)
  blocking collectives  54 us (26%)
  matrix products  22.9 us (11%)
  local copies, waits for them, and re-layouts  21.3 us (10%)
  between operations  14.9 us (7%)
  other arithmetic  2.78 us (1%)
    psum x1, blocking collectives, local(): state, mass = lax.psum((part_state, part_mass), 'ctx')  54 us
    all_gather x2, waiting for transfers between devices, gather_in_order(): pieces = lax.all_gather(pieces, axes[k])  47.8 us
    psum x1, waiting for transfers between devices, local(): state, mass = lax.psum((part_state, part_mass), 'ctx')  38.8 us
    unnamed x7, local copies, waits for them, and re-layouts  12.8 us
    dot_general x1, matrix products, local(): jnp.einsum('btw,wv->btv', mixed, whole_of(out_weight, BATCH, (0, 1), 0),...  9.14 us
    transpose x1, local copies, waits for them, and re-layouts, gather_in_order(): pieces = pieces.transpose(*back, *range(len(axes), pieces.ndim))  8.42 us
    dot_general x1, matrix products, ask_state(): jnp.einsum('bthd,bhde->bthe', features, state.astype(jnp.bfloat16), prefe...  6.56 us
    dot_general x1, matrix products, local(): jnp.einsum('bthd,bthe->bhde', key_feature, contents, preferred_element_ty...  4.4 us
  transfers between devices with their start and end apart: 3, of which 2 were waited for; matrix products, arithmetic and copies ran while one was open for 14% of the time, Pallas kernels for 0%

commit v1 on v0

v1 whole, which is shorter than its diff:
```python
import jax
import jax.numpy as jnp
from jax import lax
from jax.experimental import pallas as pl
from jax.experimental.pallas import tpu as pltpu
from jax.sharding import Mesh
from jax.sharding import PartitionSpec as P

F32, BF16 = jnp.float32, jnp.bfloat16
MESH = pl.DeviceIdType.MESH
HEADS, SIZE = 16, 128
SEQS, ROWS = 2, 256
WIDTH = HEADS * SIZE
OFFSETS = (0, 3, 1, 2)


def feature(x):
    wide = x.astype(F32)
    return jnp.where(wide > 0.0, wide + 1.0, jnp.exp(jnp.minimum(wide, 0.0)))


def kernel(
    count, q_hbm, k_hbm, v_hbm, g_hbm, w_hbm, out_hbm,
    qb, kb, vb, gb, perm, kh, vh, qh, sig, part, pmass, send1, recv1, chip, cmass, send2, recv2, xsum, xmass,
    send3, recv3, state, mixed, wbuf, outb,
    ld, osem, ya, yb, za, zb, w_send, w_core, s_send, s1, s2, s3, s4, s5,
):
    zh, y, zl, x, core = (lax.axis_index(a) for a in ("zh", "y", "zl", "x", "core"))
    other = 1 - core
    z = 2 * zh + zl
    ds = 2 * zl - 1
    zo, zi = lax.rem(z + ds + 8, 8), lax.rem(z - ds + 8, 8)
    outer = {"zh": zo // 2, "zl": lax.rem(zo, 2)}
    inner = {"zh": zi // 2, "zl": lax.rem(zi, 2)}
    ynext = [{"y": lax.rem(y + 1, 4)}, {"y": lax.rem(y + 3, 4)}]
    xpeer = [{"x": lax.rem(x + d, 4)} for d in (1, 2, 3)]
    partner = {"core": other}

    own = (zh * 4 + y) * SIZE
    wloads = [
        pltpu.make_async_copy(
            w_hbm.at[:, pl.ds(512 * n, 512)], wbuf.at[n, pl.ds(pl.multiple_of(own, SIZE), SIZE), :], ld.at[n]
        )
        for n in range(4)
    ]
    loads = [
        [pltpu.make_async_copy(h.at[s], b.at[s], ld.at[4 + 2 * i + s]) for s in range(SEQS)]
        for i, (h, b) in enumerate(((k_hbm, kb), (v_hbm, vb), (q_hbm, qb), (g_hbm, gb)))
    ]
    for c in wloads:
        c.start()
    for s in range(SEQS):
        loads[0][s].start()
        loads[1][s].start()
    for s in range(SEQS):
        loads[2][s].start()
        loads[3][s].start()

    barrier = pltpu.get_barrier_semaphore()
    for dev in (partner, outer, inner, *ynext, *xpeer):
        pl.semaphore_signal(barrier, inc=1, device_id=dev, device_id_type=MESH)
    row = lax.broadcasted_iota(jnp.int32, (256, 256), 0)
    col = lax.broadcasted_iota(jnp.int32, (256, 256), 1)
    perm[...] = jnp.where(col == (row & 15) * 16 + (row >> 4), 1.0, 0.0).astype(BF16)
    pl.semaphore_wait(barrier, 8)

    def send(src, ssem, rsem, dev, dst=None):
        pltpu.make_async_remote_copy(
            src_ref=src, dst_ref=src if dst is None else dst, send_sem=ssem, recv_sem=rsem,
            device_id=dev, device_id_type=MESH,
        ).start()

    def arrived(ref, rsem):
        pltpu.make_async_copy(ref, ref, rsem).wait()

    def piece(which, zq, yq, half=None):
        at = (lax.rem(zq + 8, 4) * 4 + lax.rem(yq + 8, 4)) * SIZE
        size = SIZE
        if half is not None:
            at, size = at + half * 64, 64
        return wbuf.at[2 * core + which, pl.ds(pl.multiple_of(at, 64), size), :]

    def share(ref):
        send(ref, w_send, w_core, partner)

    def y_full(which, zq, slot):
        ref = piece(which, zq, y)
        for d in range(2):
            send(ref, w_send, ya.at[d, 0, slot], ynext[d])

    def y_got_full(which, zq, slot):
        for d in range(2):
            yq = y - (1 - 2 * d)
            arrived(piece(which, zq, yq), ya.at[d, 0, slot])
            send(piece(which, zq, yq, d), w_send, ya.at[d, 1, slot], ynext[d])
            share(piece(which, zq, yq))

    def y_got_half(which, zq, slot):
        for d in range(2):
            ref = piece(which, zq, y + 2, d)
            arrived(ref, ya.at[d, 1, slot])
            share(ref)

    def z_own(which, yq, slot):
        send(piece(which, zh, yq), w_send, za.at[0, 0, slot], outer)

    def z_outer_full(which, yq, slot):
        ref = piece(which, zh + ds, yq)
        arrived(ref, za.at[0, 0, slot])
        send(ref, w_send, za.at[1, 0, slot], inner)
        share(ref)

    def z_inner_full(which, yq, slot):
        ref = piece(which, zh - ds, yq)
        arrived(ref, za.at[1, 0, slot])
        send(piece(which, zh - ds, yq, 1 - zl), w_send, za.at[0, 1, slot], outer)
        share(ref)

    def z_outer_half(which, yq, slot):
        ref = piece(which, zh + 2, yq, zl)
        arrived(ref, za.at[0, 1, slot])
        send(ref, w_send, za.at[1, 1, slot], inner)
        share(ref)

    def z_inner_half(which, yq, slot):
        ref = piece(which, zh + 2, yq, 1 - zl)
        arrived(ref, za.at[1, 1, slot])
        share(ref)

    for c in wloads:
        c.wait()
    y_full(0, zh, 0)
    z_own(1, y, 4)
    z_own(0, y, 0)
    y_full(1, zh, 1)

    def to_heads(left, right):
        both = jnp.concatenate([left.reshape(256, SIZE), right.reshape(256, SIZE)], axis=1)
        return jnp.dot(perm[...], both, preferred_element_type=F32)

    def sums(s):
        loads[0][s].wait()
        loads[1][s].wait()

        def some(i, mass):
            at = pl.ds(pl.multiple_of(16 * i, 16), 16)
            kf = feature(kb[s, at]).astype(BF16)
            r = to_heads(kf, vb[s, at])
            kh[:, at, :] = r[:, :SIZE].astype(BF16).reshape(HEADS, 16, SIZE)
            vh[:, at, :] = r[:, SIZE:].astype(BF16).reshape(HEADS, 16, SIZE)
            return mass + jnp.sum(kf.astype(F32), axis=0)

        mass = lax.fori_loop(0, 16, some, jnp.zeros((HEADS, SIZE), F32), unroll=2)
        pmass[s] = mass
        send1[s, pl.ds(1024, 16), :] = mass.astype(BF16)

        def one(h):
            return lax.dot_general(vh[h], kh[h], (((0,), (0,)), ((), ())), preferred_element_type=F32)

        def theirs(i, _):
            send1[s, pl.ds(pl.multiple_of(i * SIZE, SIZE), SIZE), :] = one(8 * other + i).astype(BF16)
            return 0

        lax.fori_loop(0, 8, theirs, 0, unroll=2)
        send(send1.at[s], s_send.at[s, 0], s1.at[s], partner, recv1.at[s])

        def ours(i, _):
            part[s, pl.ds(pl.multiple_of(i * SIZE, SIZE), SIZE), :] = one(8 * core + i)
            return 0

        lax.fori_loop(0, 8, ours, 0, unroll=2)

    def chip_sum(s):
        arrived(recv1.at[s], s1.at[s])
        cm = pmass[s] + recv1[s, pl.ds(1024, 16), :].astype(F32)
        cmass[s] = cm

        def group(j, _):
            at = pl.ds(pl.multiple_of(j * 256, 256), 256)
            total = part[s, at, :] + recv1[s, at, :].astype(F32)
            chip[s, at, :] = total
            send2[s, j, pl.ds(0, 256), :] = total.astype(BF16)
            send2[s, j, pl.ds(256, 16), :] = cm.astype(BF16)
            return 0

        lax.fori_loop(0, 4, group, 0)
        for d in range(3):
            send(send2.at[s, lax.rem(x + d + 1, 4)], s_send.at[s, 1 + d], s2.at[s, d], xpeer[d], recv2.at[s, d])

    def x_sum(s):
        for d in range(3):
            arrived(recv2.at[s, d], s2.at[s, d])
        total = chip[s, pl.ds(pl.multiple_of(x * 256, 256), 256), :]
        mass = cmass[s]
        for d in range(3):
            total = total + recv2[s, d, pl.ds(0, 256), :].astype(F32)
            mass = mass + recv2[s, d, pl.ds(256, 16), :].astype(F32)
        xsum[s] = total
        xmass[s] = mass
        send3[s, pl.ds(0, 256), :] = total.astype(BF16)
        send3[s, pl.ds(256, 16), :] = mass.astype(BF16)
        send(send3.at[s], s_send.at[s, 4], s3.at[s], inner, recv3.at[s])

    def blocks(s, c, xq):
        at = (8 * c + 2 * xq) * SIZE
        return state.at[s, pl.ds(pl.multiple_of(at, 256), 256), :]

    def whole_sum(s):
        arrived(recv3.at[s], s3.at[s])
        total = xsum[s] + recv3[s, pl.ds(0, 256), :].astype(F32)
        xmass[s] = (xmass[s] + recv3[s, pl.ds(256, 16), :].astype(F32)) / count
        mine = blocks(s, core, x)
        mine[...] = (total / count).astype(BF16)
        for d in range(3):
            send(mine, s_send.at[s, 5 + d], s4.at[s, d], xpeer[d])
        send(mine, s_send.at[s, 8], s5.at[s, 0], partner)

    def pass_on(s):
        for d in range(3):
            ref = blocks(s, core, lax.rem(x + 3 - d, 4))
            arrived(ref, s4.at[s, d])
            send(ref, s_send.at[s, 9 + d], s5.at[s, 1 + d], partner)

    def all_here(s):
        for d in range(4):
            arrived(blocks(s, other, lax.rem(x + 4 - d, 4)), s5.at[s, d])

    def questions(s):
        loads[2][s].wait()
        loads[3][s].wait()

        def some(i, _):
            at = pl.ds(pl.multiple_of(16 * i, 16), 16)
            r = to_heads(feature(qb[s, at]).astype(BF16), gb[s, at])
            qh[s, :, at, :] = r[:, :SIZE].astype(BF16).reshape(HEADS, 16, SIZE)
            gate = (count**0.5) / (1.0 + jnp.exp(-r[:, SIZE:]))
            sig[s, :, at, :] = gate.reshape(HEADS, 16, SIZE)
            return 0

        lax.fori_loop(0, 16, some, 0, unroll=2)

    def answers(s):
        def one(h, _):
            at = pl.ds(pl.multiple_of(h * SIZE, SIZE), SIZE)
            row = xmass[s, pl.ds(h, 1), :].astype(BF16)
            right = jnp.concatenate([state[s, at, :], jnp.broadcast_to(row, (SIZE, SIZE))], axis=0)
            r = lax.dot_general(qh[s, h], right, (((1,), (1,)), ((), ())), preferred_element_type=F32)
            read = r[:, :SIZE] * sig[s, h] / (r[:, SIZE:] + 0.001)
            mixed[pl.ds(s * ROWS, ROWS), at] = read.astype(BF16)
            return 0

        lax.fori_loop(0, HEADS, one, 0, unroll=2)

    sums(0)
    sums(1)
    y_got_full(0, zh, 0)
    z_own(0, y - 1, 1)
    z_own(0, y + 1, 2)
    z_outer_full(1, y, 4)
    y_full(1, zh + ds, 2)
    chip_sum(0)
    z_outer_full(0, y, 0)
    chip_sum(1)
    y_got_full(1, zh, 1)
    y_got_half(0, zh, 0)
    z_own(0, y + 2, 3)
    z_inner_full(1, y, 4)
    y_full(1, zh - ds, 3)
    questions(0)
    x_sum(0)
    z_inner_full(0, y, 0)
    z_outer_full(0, y - 1, 1)
    z_outer_half(1, y, 4)
    questions(1)
    x_sum(1)
    whole_sum(0)
    z_outer_full(0, y + 1, 2)
    z_inner_full(0, y - 1, 1)
    z_inner_half(1, y, 4)
    y_full(1, zh + 2, 4)
    y_got_full(1, zh + ds, 2)
    y_got_full(1, zh - ds, 3)
    whole_sum(1)
    pass_on(0)
    z_outer_full(0, y + 2, 3)
    z_inner_full(0, y + 1, 2)
    y_got_half(1, zh, 1)
    all_here(0)
    answers(0)
    z_inner_full(0, y + 2, 3)
    y_got_half(1, zh + ds, 2)
    pass_on(1)
    y_got_full(1, zh + 2, 4)
    all_here(1)
    answers(1)
    for slot in range(4):
        z_outer_half(0, y + OFFSETS[slot], slot)
    y_got_half(1, zh - ds, 3)
    for slot in range(4):
        z_inner_half(0, y + OFFSETS[slot], slot)
    y_got_half(1, zh + 2, 4)

    sized = wbuf.at[pl.ds(0, 2), pl.ds(0, 15 * SIZE), :]
    arrived(sized, w_core)

    stores = []
    for n in range(4):
        for s in range(SEQS):
            at = pl.ds(s * ROWS, ROWS)
            o = jnp.dot(mixed[at, :], wbuf[n], preferred_element_type=F32)
            outb[s, :, pl.ds(512 * n, 512)] = o.astype(BF16)
            c = pltpu.make_async_copy(
                outb.at[s, :, pl.ds(512 * n, 512)], out_hbm.at[s, :, pl.ds(512 * n, 512)], osem.at[2 * n + s]
            )
            c.start()
            stores.append(c)

    everything = wbuf.at[:, pl.ds(0, 15 * SIZE), :]
    arrived(everything, w_send)
    for s in range(SEQS):
        arrived(send1.at[s], s_send.at[s, 0])
        for d in range(3):
            arrived(send2.at[s, d], s_send.at[s, 1 + d])
        arrived(send3.at[s], s_send.at[s, 4])
        for d in range(7):
            arrived(blocks(s, core, x), s_send.at[s, 5 + d])
    for c in stores:
        c.wait()


def solution(mesh):
    finer = Mesh(mesh.devices.reshape(4, 4, 2, 4, 2), ("zh", "y", "zl", "x", "core"))
    batch, ctx = ("zh", "y"), ("zl", "x", "core")

    def local(asked_for, offered, contents, gate_rows, out_weight):
        count = float(asked_for.shape[1] * 16)
        dma = pltpu.SemaphoreType.DMA
        vm = pltpu.VMEM
        block = (SEQS, ROWS, HEADS, SIZE)
        return pl.pallas_call(
            lambda *refs: kernel(count, *refs),
            out_shape=jax.ShapeDtypeStruct((SEQS, ROWS, WIDTH), BF16),
            in_specs=[pl.BlockSpec(memory_space=pl.ANY)] * 5,
            out_specs=pl.BlockSpec(memory_space=pl.ANY),
            scratch_shapes=[
                vm(block, BF16), vm(block, BF16), vm(block, BF16), vm(block, BF16),
                vm((256, 256), BF16),
                vm((HEADS, ROWS, SIZE), BF16), vm((HEADS, ROWS, SIZE), BF16),
                vm((SEQS, HEADS, ROWS, SIZE), BF16), vm((SEQS, HEADS, ROWS, SIZE), F32),
                vm((SEQS, 1024, SIZE), F32), vm((SEQS, HEADS, SIZE), F32),
                vm((SEQS, 1040, SIZE), BF16), vm((SEQS, 1040, SIZE), BF16),
                vm((SEQS, 1024, SIZE), F32), vm((SEQS, HEADS, SIZE), F32),
                vm((SEQS, 4, 272, SIZE), BF16), vm((SEQS, 3, 272, SIZE), BF16),
                vm((SEQS, 256, SIZE), F32), vm((SEQS, HEADS, SIZE), F32),
                vm((SEQS, 272, SIZE), BF16), vm((SEQS, 272, SIZE), BF16),
                vm((SEQS, WIDTH, SIZE), BF16),
                vm((SEQS * ROWS, WIDTH), BF16),
                vm((4, WIDTH, 512), BF16),
                vm((SEQS, ROWS, WIDTH), BF16),
                dma((12,)), dma((8,)),
                dma((2, 2, 5)), dma((1,)), dma((2, 2, 5)), dma((1,)),
                dma, dma, dma((SEQS, 12)),
                dma((SEQS,)), dma((SEQS, 3)), dma((SEQS,)), dma((SEQS, 3)), dma((SEQS, 4)),
            ],
            compiler_params=pltpu.CompilerParams(
                collective_id=0, has_side_effects=True, vmem_limit_bytes=60 * 1024 * 1024
            ),
        )(asked_for, offered, contents, gate_rows, out_weight)

    cut = P(batch, ctx, None, None)
    return jax.shard_map(
        local, mesh=finer, in_specs=(cut, cut, cut, cut, P(batch, None)), out_specs=P(batch, ctx, None), check_vma=False
    )
```

time: 204 us -> 62.1 us (0.30)
  waiting for transfers between devices: 87.3 us -> 0 us
  Pallas kernels: 0 us -> 58.8 us
  blocking collectives: 54 us -> 0 us
  matrix products: 22.9 us -> 0 us
  local copies, waits for them, and re-layouts: 21.3 us -> 3.16 us
  between operations: 14.9 us -> 0.01 us
  other arithmetic: 2.78 us -> 0 us
    pallas_call x0 -> x1, Pallas kernels: none -> 58.8 us  [local(): pl.pallas_call(lambda *refs: kernel(count, *refs), out_shape=jax.ShapeDty...]
    psum x1 -> x0, blocking collectives: 54 us -> none  [local(): state, mass = lax.psum((part_state, part_mass), 'ctx')]
    all_gather x2 -> x0, waiting for transfers between devices: 47.8 us -> none  [gather_in_order(): pieces = lax.all_gather(pieces, axes[k])]
    psum x1 -> x0, waiting for transfers between devices: 38.8 us -> none  [local(): state, mass = lax.psum((part_state, part_mass), 'ctx')]
    dot_general x4 -> x0, matrix products: 22.9 us -> none  [the longest x1 9.14 us: local(): jnp.einsum('btw,wv->btv', mixed, whole_of(out_weight, BATCH, (0, 1), 0),...]
    unnamed x7 -> x1, local copies, waits for them, and re-layouts: 12.8 us -> 3.16 us
    transpose x1 -> x0, local copies, waits for them, and re-layouts: 8.42 us -> none  [gather_in_order(): pieces = pieces.transpose(*back, *range(len(axes), pieces.ndim))]
    reduce_sum x1 -> x0, other arithmetic: 2.77 us -> none  [local(): part_mass = jnp.sum(key_feature.astype(jnp.float32), axis=1)]
  transfers between devices with their start and end apart: 3 -> 0, of which waited for: 2 -> 0; matrix products, arithmetic and copies ran while one was open for 14% -> 0% of each run, Pallas kernels for 0% -> 0%
where the time goes in v1:
time: 62.1 us; the launch traced here: 62 us
  Pallas kernels  58.8 us (95%)
  local copies, waits for them, and re-layouts  3.16 us (5%)
    pallas_call x1, Pallas kernels, local(): pl.pallas_call(lambda *refs: kernel(count, *refs), out_shape=jax.ShapeDty...  58.8 us
    unnamed x1, local copies, waits for them, and re-layouts  3.16 us

profile of v1, /device:TPU:1, one launch (start us, length us, event | category | flops | bytes accessed | tf_op | source)
XLA Modules:
  0.0 62.0 jit_solution(13891006858160106939)
XLA Ops:
  0.0 58.8 %shard_map.55 = bf16[2,256,2048]{2,1,0:T(8,128)(2,1)} custom-call(bf16[2,256,16,128]{3,2,1,0:T(8,128)(2,1)} %refs_0_.1, bf16[2,256,16,128]{3,2,1,0:T(8,128)(2,1)} %refs_1_.1, bf16[2,256,16,128]{3,2,1,0:T(8,128)(2,1)} %refs_2_.1, bf16[2,256,16,128]{3,2,1,0:T(8,128)(2,1)} %refs_3_.1, bf16[128,2048]{1,0:T(8,128)(2,1)} %refs_4_.1), custom_call_target="tpu_custom_call" | custom-call | tf_op jit(solution)/shard_map/pallas_call | solution.py:340
  58.8 3.2 %copy.7 = bf16[2,256,2048]{2,1,0:T(8,128)(2,1)} copy(bf16[2,256,2048]{2,1,0:T(8,128)(2,1)} %shard_map.55) | data formatting | bytes 4194304

commit v2 on v1

v2 whole, which is shorter than its diff:
```python
import jax
import jax.numpy as jnp
from jax import lax
from jax.experimental import pallas as pl
from jax.experimental.pallas import tpu as pltpu
from jax.sharding import Mesh
from jax.sharding import PartitionSpec as P

F32, BF16 = jnp.float32, jnp.bfloat16
MESH = pl.DeviceIdType.MESH
HEADS, SIZE = 16, 128
SEQS, ROWS = 2, 256
WIDTH = HEADS * SIZE
HALF = SIZE // 2
UN, UK = 8, 4
OFFSETS = (0, 3, 1, 2, 0)
PEERS = (2, 1, 3)


def feature(x):
    wide = x.astype(F32)
    return jnp.where(wide > 0.0, wide + 1.0, jnp.exp(jnp.minimum(wide, 0.0)))


def kernel(
    count, q_hbm, k_hbm, v_hbm, g_hbm, w_hbm, out,
    qb, kb, vb, gb, perm, kh, vh, qh, sig, part, pmass, send1, recv1, chip, send2, recv2, xsum, mass,
    send3, recv3, state, mixed, wbuf,
    ld, ya, za, w_send, w_core, s_send, s1, s2, s3, s4, s5,
):
    zh, y, zl, x, core = (lax.axis_index(a) for a in ("zh", "y", "zl", "x", "core"))
    other = 1 - core
    z = 2 * zh + zl
    ds = 2 * zl - 1
    zo, zi = lax.rem(z + ds + 8, 8), lax.rem(z - ds + 8, 8)
    outer = {"zh": zo // 2, "zl": lax.rem(zo, 2)}
    inner = {"zh": zi // 2, "zl": lax.rem(zi, 2)}
    ynext = [{"y": lax.rem(y + 1, 4)}, {"y": lax.rem(y + 3, 4)}]
    peers = [{"x": lax.rem(x + b, 4)} for b in PEERS]
    partner = {"core": other}

    own = (zh * 4 + y) * SIZE
    wloads = [
        pltpu.make_async_copy(
            w_hbm.at[:, pl.ds(512 * n, 512)], wbuf.at[n, pl.ds(pl.multiple_of(own, SIZE), SIZE), :], ld.at[n]
        )
        for n in range(4)
    ]
    loads = [
        [pltpu.make_async_copy(h.at[s], b.at[s], ld.at[4 + 2 * i + s]) for s in range(SEQS)]
        for i, (h, b) in enumerate(((k_hbm, kb), (v_hbm, vb), (q_hbm, qb), (g_hbm, gb)))
    ]
    for c in wloads:
        c.start()
    for s in range(SEQS):
        loads[0][s].start()
        loads[1][s].start()
    for s in range(SEQS):
        loads[2][s].start()
        loads[3][s].start()

    barrier = pltpu.get_barrier_semaphore()
    for dev in (partner, outer, inner, *ynext, *peers):
        pl.semaphore_signal(barrier, inc=1, device_id=dev, device_id_type=MESH)
    row = lax.broadcasted_iota(jnp.int32, (256, 256), 0)
    col = lax.broadcasted_iota(jnp.int32, (256, 256), 1)
    perm[...] = jnp.where(col == (row & 15) * 16 + (row >> 4), 1.0, 0.0).astype(BF16)
    pl.semaphore_wait(barrier, 8)

    def send(src, ssem, rsem, dev, dst=None):
        pltpu.make_async_remote_copy(
            src_ref=src, dst_ref=src if dst is None else dst, send_sem=ssem, recv_sem=rsem,
            device_id=dev, device_id_type=MESH,
        ).start()

    def arrived(ref, rsem):
        pltpu.make_async_copy(ref, ref, rsem).wait()

    def piece(which, zq, yq, u):
        at = (lax.rem(zq + 8, 4) * 4 + lax.rem(yq + 8, 4)) * SIZE + u * HALF
        return wbuf.at[2 * core + which, pl.ds(pl.multiple_of(at, HALF), HALF), :]

    def share(ref):
        send(ref, w_send, w_core, partner)

    y_zq = (zh, zh, zh + ds, zh - ds, zh + 2)
    y_half = ((0, 1), (0, 1), (zl, 1 - zl), (1 - zl, zl), (zl, 1 - zl))

    def y_send(which, slot, d, u):
        send(piece(which, y_zq[slot], y, u), w_send, ya.at[d, 0, slot, u], ynext[d])

    def y_got_full(which, slot, d, f):
        u = y_half[slot][f]
        ref = piece(which, y_zq[slot], y - (1 - 2 * d), u)
        arrived(ref, ya.at[d, 0, slot, u])

        def onward():
            send(ref, w_send, ya.at[d, 1, slot, 0], ynext[d])

        if slot < 2:
            if u == d:
                onward()
        else:
            pl.when(u == d)(onward)
        share(ref)
        if which == 0:
            z_own(0, 1 + d, u)

    def y_got_half(which, slot, d):
        ref = piece(which, y_zq[slot], y + 2, d)
        arrived(ref, ya.at[d, 1, slot, 0])
        share(ref)
        if which == 0:
            z_own(0, 3, d)

    def z_own(which, slot, u):
        send(piece(which, zh, y + OFFSETS[slot], u), w_send, za.at[0, 0, slot, u], outer)

    def to_y(which, slot, u):
        if which == 1:
            for d in range(2):
                y_send(1, slot, d, u)

    def outer_full(which, slot, f):
        u = (zl, 1 - zl)[f]
        ref = piece(which, zh + ds, y + OFFSETS[slot], u)
        arrived(ref, za.at[0, 0, slot, u])
        send(ref, w_send, za.at[1, 0, slot, u], inner)
        to_y(which, 2, u)
        share(ref)

    def inner_full(which, slot, f):
        u = (1 - zl, zl)[f]
        ref = piece(which, zh - ds, y + OFFSETS[slot], u)
        arrived(ref, za.at[1, 0, slot, u])
        if f == 0:
            send(ref, w_send, za.at[0, 1, slot, 0], outer)
        to_y(which, 3, u)
        share(ref)

    def outer_half(which, slot):
        ref = piece(which, zh + 2, y + OFFSETS[slot], zl)
        arrived(ref, za.at[0, 1, slot, 0])
        send(ref, w_send, za.at[1, 1, slot, 0], inner)
        to_y(which, 4, zl)
        share(ref)

    def inner_half(which, slot):
        ref = piece(which, zh + 2, y + OFFSETS[slot], 1 - zl)
        arrived(ref, za.at[1, 1, slot, 0])
        to_y(which, 4, 1 - zl)
        share(ref)

    for c in wloads:
        c.wait()
    for f in range(2):
        for d in range(2):
            y_send(0, 0, d, (d, 1 - d)[f])
        z_own(1, 4, (1 - zl, zl)[f])
    for f in range(2):
        z_own(0, 0, (1 - zl, zl)[f])
        for d in range(2):
            y_send(1, 1, d, (d, 1 - d)[f])

    def to_heads(left, right):
        both = jnp.concatenate([left.reshape(256, SIZE), right.reshape(256, SIZE)], axis=1)
        return jnp.dot(perm[...], both, preferred_element_type=F32)

    def keys(s, part_of):
        if part_of == 0:
            loads[0][s].wait()
            loads[1][s].wait()

        def some(i, total):
            at = pl.ds(pl.multiple_of(16 * i, 16), 16)
            kf = feature(kb[s, at]).astype(BF16)
            r = to_heads(kf, vb[s, at])
            kh[:, at, :] = r[:, :SIZE].astype(BF16).reshape(HEADS, 16, SIZE)
            vh[:, at, :] = r[:, SIZE:].astype(BF16).reshape(HEADS, 16, SIZE)
            return total + jnp.sum(kf.astype(F32), axis=0)

        start = jnp.zeros((HEADS, SIZE), F32) if part_of == 0 else pmass[s]
        total = lax.fori_loop(8 * part_of, 8 * part_of + 8, some, start, unroll=UK)
        pmass[s] = total
        if part_of == 1:
            send1[s, pl.ds(1024, 16), :] = total.astype(BF16)

    def product(h):
        return lax.dot_general(
            vh[h, pl.ds(0, ROWS), :], kh[h, pl.ds(0, ROWS), :], (((0,), (0,)), ((), ())), preferred_element_type=F32
        )

    def theirs(s):
        def one(i, _):
            send1[s, pl.ds(pl.multiple_of(i * SIZE, SIZE), SIZE), :] = product(8 * other + i).astype(BF16)
            return 0

        lax.fori_loop(0, 8, one, 0, unroll=UN)
        send(send1.at[s], s_send.at[s, 0], s1.at[s], partner, recv1.at[s])

    def ours(s):
        def one(i, _):
            part[s, pl.ds(pl.multiple_of(i * SIZE, SIZE), SIZE), :] = product(8 * core + i)
            return 0

        lax.fori_loop(0, 8, one, 0, unroll=UN)

    def chip_sum(s):
        arrived(recv1.at[s], s1.at[s])
        cm = pmass[s] + recv1[s, pl.ds(1024, 16), :].astype(F32)
        mass[s] = cm

        def one(j, _):
            at = pl.ds(pl.multiple_of(j * 256, 256), 256)
            total = part[s, at, :] + recv1[s, at, :].astype(F32)
            chip[s, at, :] = total
            send2[s, j, pl.ds(0, 256), :] = total.astype(BF16)
            send2[s, j, pl.ds(256, 16), :] = cm.astype(BF16)
            return 0

        lax.fori_loop(0, 4, one, 0)
        for k, b in enumerate(PEERS):
            send(send2.at[s, lax.rem(x + b, 4)], s_send.at[s, 1 + k], s2.at[s, k], peers[k], recv2.at[s, k])

    def pair_of(s, xq):
        return state.at[s, pl.ds(pl.multiple_of((8 * core + 2 * xq) * SIZE, 256), 256), :]

    def x_sum(s):
        total = chip[s, pl.ds(pl.multiple_of(x * 256, 256), 256), :]
        m = mass[s]
        for k in range(3):
            arrived(recv2.at[s, k], s2.at[s, k])
            total = total + recv2[s, k, pl.ds(0, 256), :].astype(F32)
            m = m + recv2[s, k, pl.ds(256, 16), :].astype(F32)
        xsum[s] = total
        mass[s] = m
        send3[s, pl.ds(0, 256), :] = total.astype(BF16)
        send3[s, pl.ds(256, 16), :] = m.astype(BF16)
        send(send3.at[s], s_send.at[s, 4], s3.at[s], inner, recv3.at[s])

    def whole_sum(s):
        arrived(recv3.at[s], s3.at[s])
        mass[s] = (mass[s] + recv3[s, pl.ds(256, 16), :].astype(F32)) / count
        mine = pair_of(s, x)
        mine[...] = ((xsum[s] + recv3[s, pl.ds(0, 256), :].astype(F32)) / count).astype(BF16)
        for k in range(3):
            send(mine, s_send.at[s, 5 + k], s4.at[s, k], peers[k])

    def pass_on(s):
        for k, b in enumerate(PEERS):
            arrived(pair_of(s, lax.rem(x + 4 - b, 4)), s4.at[s, k])
        ref = state.at[s, pl.ds(pl.multiple_of(8 * core * SIZE, SIZE), 8 * SIZE), :]
        send(ref, s_send.at[s, 8], s5.at[s], partner)

    def questions(s, part_of):
        if part_of == 0:
            loads[2][s].wait()
            loads[3][s].wait()

        def some(i, _):
            at = pl.ds(pl.multiple_of(16 * i, 16), 16)
            r = to_heads(feature(qb[s, at]).astype(BF16), gb[s, at])
            qh[s, :, at, :] = r[:, :SIZE].astype(BF16).reshape(HEADS, 16, SIZE)
            gate = (count**0.5) / (1.0 + jnp.exp(-r[:, SIZE:]))
            sig[s, :, at, :] = gate.reshape(HEADS, 16, SIZE)
            return 0

        lax.fori_loop(8 * part_of, 8 * part_of + 8, some, 0, unroll=UK)

    def answers(s, side):
        if side is other:
            arrived(state.at[s, pl.ds(pl.multiple_of(8 * other * SIZE, SIZE), 8 * SIZE), :], s5.at[s])

        def one(i, _):
            h = 8 * side + i
            at = pl.ds(pl.multiple_of(h * SIZE, SIZE), SIZE)
            row = mass[s, pl.ds(h, 1), :].astype(BF16)
            right = jnp.concatenate([state[s, at, :], jnp.broadcast_to(row, (SIZE, SIZE))], axis=0)
            r = lax.dot_general(
                qh[s, h, pl.ds(0, ROWS), :], right, (((1,), (1,)), ((), ())), preferred_element_type=F32
            )
            read = r[:, :SIZE] * sig[s, h, pl.ds(0, ROWS), :] / (r[:, SIZE:] + 0.001)
            mixed[pl.ds(s * ROWS, ROWS), at] = read.astype(BF16)
            return 0

        lax.fori_loop(0, 8, one, 0, unroll=UN)

    keys(0, 0)
    keys(0, 1)
    theirs(0)
    ours(0)
    keys(1, 0)
    keys(1, 1)
    y_got_full(0, 0, 0, 0)
    y_got_full(0, 0, 1, 1)
    outer_full(1, 4, 0)
    chip_sum(0)
    theirs(1)
    ours(1)
    questions(0, 0)
    y_got_full(0, 0, 0, 1)
    y_got_full(0, 0, 1, 0)
    outer_full(1, 4, 1)
    questions(0, 1)
    chip_sum(1)
    questions(1, 0)
    outer_full(0, 0, 0)
    y_got_full(1, 1, 0, 0)
    y_got_full(1, 1, 1, 1)
    questions(1, 1)
    inner_full(1, 4, 0)
    outer_full(0, 0, 1)
    y_got_full(1, 1, 0, 1)
    y_got_full(1, 1, 1, 0)
    inner_full(1, 4, 1)
    y_got_half(0, 0, 0)
    outer_full(0, 1, 0)
    y_got_half(0, 0, 1)
    x_sum(0)
    outer_full(0, 2, 1)
    y_got_full(1, 2, 0, 0)
    y_got_full(1, 2, 1, 0)
    inner_full(0, 0, 0)
    outer_full(0, 1, 1)
    y_got_full(1, 2, 0, 1)
    y_got_full(1, 2, 1, 1)
    inner_full(0, 0, 1)
    x_sum(1)
    outer_full(0, 2, 0)
    y_got_half(1, 1, 0)
    y_got_half(1, 1, 1)
    inner_full(0, 1, 0)
    outer_half(1, 4)
    y_got_full(1, 3, 0, 0)
    y_got_full(1, 3, 1, 0)
    whole_sum(0)
    y_got_full(1, 3, 0, 1)
    y_got_full(1, 3, 1, 1)
    outer_full(0, 3, 0)
    inner_full(0, 2, 1)
    outer_full(0, 3, 1)
    y_got_half(1, 2, 0)
    y_got_half(1, 2, 1)
    inner_full(0, 1, 1)
    outer_half(0, 0)
    y_got_full(1, 4, 0, 0)
    y_got_full(1, 4, 1, 0)
    whole_sum(1)
    outer_half(0, 1)
    y_got_half(1, 3, 0)
    y_got_half(1, 3, 1)
    inner_full(0, 2, 0)
    pass_on(0)
    answers(0, core)
    inner_half(1, 4)
    answers(0, other)
    inner_full(0, 3, 0)
    outer_half(0, 2)
    inner_full(0, 3, 1)
    pass_on(1)
    answers(1, core)
    y_got_full(1, 4, 0, 1)
    y_got_full(1, 4, 1, 1)
    inner_half(0, 0)
    answers(1, other)
    outer_half(0, 3)
    inner_half(0, 1)
    inner_half(0, 2)
    y_got_half(1, 4, 0)
    y_got_half(1, 4, 1)
    inner_half(0, 3)

    def project(n, s):
        o = jnp.dot(mixed[pl.ds(s * ROWS, ROWS), :], wbuf[n], preferred_element_type=F32)
        at = pl.ds(pl.multiple_of(512 * n, 512), 512)
        out[s, :, at] = o.astype(BF16)

    for i in range(2):
        for s in range(SEQS):
            project(2 * core + i, s)
    arrived(wbuf.at[pl.ds(0, 2), pl.ds(0, 15 * SIZE), :], w_core)
    for i in range(2):
        for s in range(SEQS):
            project(2 * other + i, s)

    arrived(wbuf.at[:, pl.ds(0, 15 * SIZE), :], w_send)
    for s in range(SEQS):
        arrived(send1.at[s], s_send.at[s, 0])
        for k in range(3):
            arrived(send2.at[s, 0], s_send.at[s, 1 + k])
            arrived(pair_of(s, x), s_send.at[s, 5 + k])
        arrived(send3.at[s], s_send.at[s, 4])
        arrived(state.at[s, pl.ds(0, 8 * SIZE), :], s_send.at[s, 8])


def solution(mesh):
    finer = Mesh(mesh.devices.reshape(4, 4, 2, 4, 2), ("zh", "y", "zl", "x", "core"))
    batch, ctx = ("zh", "y"), ("zl", "x", "core")

    def local(asked_for, offered, contents, gate_rows, out_weight):
        count = float(asked_for.shape[1] * 16)
        dma = pltpu.SemaphoreType.DMA
        vm = pltpu.VMEM
        block = (SEQS, ROWS, HEADS, SIZE)
        return pl.pallas_call(
            lambda *refs: kernel(count, *refs),
            out_shape=jax.ShapeDtypeStruct((SEQS, ROWS, WIDTH), BF16),
            in_specs=[pl.BlockSpec(memory_space=pltpu.HBM)] * 5,
            out_specs=pl.BlockSpec(memory_space=pltpu.VMEM),
            scratch_shapes=[
                vm(block, BF16), vm(block, BF16), vm(block, BF16), vm(block, BF16),
                vm((256, 256), BF16),
                vm((HEADS, ROWS + 16, SIZE), BF16), vm((HEADS, ROWS + 16, SIZE), BF16),
                vm((SEQS, HEADS, ROWS + 16, SIZE), BF16), vm((SEQS, HEADS, ROWS + 8, SIZE), F32),
                vm((SEQS, 1024, SIZE), F32), vm((SEQS, HEADS, SIZE), F32),
                vm((SEQS, 1040, SIZE), BF16), vm((SEQS, 1040, SIZE), BF16),
                vm((SEQS, 1024, SIZE), F32),
                vm((SEQS, 4, 272, SIZE), BF16), vm((SEQS, 3, 272, SIZE), BF16),
                vm((SEQS, 256, SIZE), F32), vm((SEQS, HEADS, SIZE), F32),
                vm((SEQS, 272, SIZE), BF16), vm((SEQS, 272, SIZE), BF16),
                vm((SEQS, WIDTH, SIZE), BF16),
                vm((SEQS * ROWS, WIDTH), BF16),
                vm((4, WIDTH, 512), BF16),
                dma((12,)),
                dma((2, 2, 5, 2)), dma((2, 2, 5, 2)),
                dma, dma, dma((SEQS, 9)),
                dma((SEQS,)), dma((SEQS, 3)), dma((SEQS,)), dma((SEQS, 3)), dma((SEQS,)),
            ],
            compiler_params=pltpu.CompilerParams(
                collective_id=0, has_side_effects=True, vmem_limit_bytes=44 * 1024 * 1024
            ),
        )(*(pltpu.with_memory_space_constraint(a, pltpu.HBM) for a in (asked_for, offered, contents, gate_rows, out_weight)))

    cut = P(batch, ctx, None, None)
    return jax.shard_map(
        local, mesh=finer, in_specs=(cut, cut, cut, cut, P(batch, None)), out_specs=P(batch, ctx, None), check_vma=False
    )
```

time: 62.1 us -> 48 us (0.77)
  Pallas kernels: 58.8 us -> 46.6 us
  local copies, waits for them, and re-layouts: 3.16 us -> 1.32 us
    pallas_call x1, Pallas kernels: 58.8 us -> 46.6 us  [local(): pl.pallas_call(lambda *refs: kernel(count, *refs), out_shape=jax.ShapeDty...]
    unnamed x1, local copies, waits for them, and re-layouts: 3.16 us -> 1.32 us
where the time goes in v2:
time: 48 us; the launch traced here: 47.9 us
  Pallas kernels  46.6 us (97%)
  local copies, waits for them, and re-layouts  1.32 us (3%)
    pallas_call x1, Pallas kernels, local(): pl.pallas_call(lambda *refs: kernel(count, *refs), out_shape=jax.ShapeDty...  46.6 us
    unnamed x1, local copies, waits for them, and re-layouts  1.32 us

profile of v2, /device:TPU:1, one launch (start us, length us, event | category | flops | bytes accessed | tf_op | source)
XLA Modules:
  0.0 47.9 jit_solution(9606046400475001355)
XLA Ops:
  0.0 46.6 %shard_map.55 = bf16[2,256,2048]{2,1,0:T(8,128)(2,1)S(1)} custom-call(bf16[2,256,16,128]{3,2,1,0:T(8,128)(2,1)} %refs_0_.1, bf16[2,256,16,128]{3,2,1,0:T(8,128)(2,1)} %refs_1_.1, bf16[2,256,16,128]{3,2,1,0:T(8,128)(2,1)} %refs_2_.1, bf16[2,256,16,128]{3,2,1,0:T(8,128)(2,1)} %refs_3_.1, bf16[128,2048]{1,0:T(8,128)(2,1)} %refs_4_.1), custom_call_target="tpu_custom_call" | custom-call | tf_op jit(solution)/shard_map/pallas_call | solution.py:405
  46.6 1.3 %copy.7 = bf16[2,256,2048]{2,1,0:T(8,128)(2,1)} copy(bf16[2,256,2048]{2,1,0:T(8,128)(2,1)S(1)} %shard_map.55) | data formatting | bytes 4194304

commit v3 on v2

--- a/solution.py
+++ b/solution.py
@@ -12,6 +12,7 @@
 SEQS, ROWS = 2, 256
 WIDTH = HEADS * SIZE
 HALF = SIZE // 2
+CUT = 384
 UN, UK = 8, 4
 OFFSETS = (0, 3, 1, 2, 0)
 PEERS = (2, 1, 3)
@@ -25,7 +26,7 @@
 def kernel(
     count, q_hbm, k_hbm, v_hbm, g_hbm, w_hbm, out,
     qb, kb, vb, gb, perm, kh, vh, qh, sig, part, pmass, send1, recv1, chip, send2, recv2, xsum, mass,
-    send3, recv3, state, mixed, wbuf,
+    send3, recv3, state, mixed, wa, wb, acca, accb,
     ld, ya, za, w_send, w_core, s_send, s1, s2, s3, s4, s5,
 ):
     zh, y, zl, x, core = (lax.axis_index(a) for a in ("zh", "y", "zl", "x", "core"))
@@ -40,11 +41,16 @@
     partner = {"core": other}
 
     own = (zh * 4 + y) * SIZE
+    wbuf, acc = (wa, wb), (acca, accb)
+    block_cols = ((0, CUT), (CUT, 1024 - CUT))
     wloads = [
         pltpu.make_async_copy(
-            w_hbm.at[:, pl.ds(512 * n, 512)], wbuf.at[n, pl.ds(pl.multiple_of(own, SIZE), SIZE), :], ld.at[n]
+            w_hbm.at[:, pl.ds(1024 * c + block_cols[which][0], block_cols[which][1])],
+            wbuf[which].at[c, pl.ds(pl.multiple_of(own, SIZE), SIZE), :],
+            ld.at[2 * c + which],
         )
-        for n in range(4)
+        for which in range(2)
+        for c in range(2)
     ]
     loads = [
         [pltpu.make_async_copy(h.at[s], b.at[s], ld.at[4 + 2 * i + s]) for s in range(SEQS)]
@@ -78,16 +84,16 @@
 
     def piece(which, zq, yq, u):
         at = (lax.rem(zq + 8, 4) * 4 + lax.rem(yq + 8, 4)) * SIZE + u * HALF
-        return wbuf.at[2 * core + which, pl.ds(pl.multiple_of(at, HALF), HALF), :]
-
-    def share(ref):
-        send(ref, w_send, w_core, partner)
+        return wbuf[which].at[core, pl.ds(pl.multiple_of(at, HALF), HALF), :]
+
+    def share(ref, which, group):
+        send(ref, w_send.at[which], w_core.at[which, group], partner)
 
     y_zq = (zh, zh, zh + ds, zh - ds, zh + 2)
     y_half = ((0, 1), (0, 1), (zl, 1 - zl), (1 - zl, zl), (zl, 1 - zl))
 
     def y_send(which, slot, d, u):
-        send(piece(which, y_zq[slot], y, u), w_send, ya.at[d, 0, slot, u], ynext[d])
+        send(piece(which, y_zq[slot], y, u), w_send.at[which], ya.at[d, 0, slot, u], ynext[d])
 
     def y_got_full(which, slot, d, f):
         u = y_half[slot][f]
@@ -95,26 +101,26 @@
         arrived(ref, ya.at[d, 0, slot, u])
 
         def onward():
-            send(ref, w_send, ya.at[d, 1, slot, 0], ynext[d])
+            send(ref, w_send.at[which], ya.at[d, 1, slot, 0], ynext[d])
 
         if slot < 2:
             if u == d:
                 onward()
         else:
             pl.when(u == d)(onward)
-        share(ref)
+        share(ref, which, (0, 0, 1, 2, 3)[slot])
         if which == 0:
             z_own(0, 1 + d, u)
 
     def y_got_half(which, slot, d):
         ref = piece(which, y_zq[slot], y + 2, d)
         arrived(ref, ya.at[d, 1, slot, 0])
-        share(ref)
+        share(ref, which, (0, 0, 1, 2, 3)[slot])
         if which == 0:
             z_own(0, 3, d)
 
     def z_own(which, slot, u):
-        send(piece(which, zh, y + OFFSETS[slot], u), w_send, za.at[0, 0, slot, u], outer)
+        send(piece(which, zh, y + OFFSETS[slot], u), w_send.at[which], za.at[0, 0, slot, u], outer)
 
     def to_y(which, slot, u):
         if which == 1:
@@ -125,31 +131,31 @@
         u = (zl, 1 - zl)[f]
         ref = piece(which, zh + ds, y + OFFSETS[slot], u)
         arrived(ref, za.at[0, 0, slot, u])
-        send(ref, w_send, za.at[1, 0, slot, u], inner)
+        send(ref, w_send.at[which], za.at[1, 0, slot, u], inner)
         to_y(which, 2, u)
-        share(ref)
+        share(ref, which, 1)
 
     def inner_full(which, slot, f):
         u = (1 - zl, zl)[f]
         ref = piece(which, zh - ds, y + OFFSETS[slot], u)
         arrived(ref, za.at[1, 0, slot, u])
         if f == 0:
-            send(ref, w_send, za.at[0, 1, slot, 0], outer)
+            send(ref, w_send.at[which], za.at[0, 1, slot, 0], outer)
         to_y(which, 3, u)
-        share(ref)
+        share(ref, which, 2)
 
     def outer_half(which, slot):
         ref = piece(which, zh + 2, y + OFFSETS[slot], zl)
         arrived(ref, za.at[0, 1, slot, 0])
-        send(ref, w_send, za.at[1, 1, slot, 0], inner)
+        send(ref, w_send.at[which], za.at[1, 1, slot, 0], inner)
         to_y(which, 4, zl)
-        share(ref)
+        share(ref, which, 3)
 
     def inner_half(which, slot):
         ref = piece(which, zh + 2, y + OFFSETS[slot], 1 - zl)
         arrived(ref, za.at[1, 1, slot, 0])
         to_y(which, 4, 1 - zl)
-        share(ref)
+        share(ref, which, 3)
 
     for c in wloads:
         c.wait()
@@ -285,105 +291,117 @@
 
         lax.fori_loop(0, 8, one, 0, unroll=UN)
 
+    def project(group, side):
+        groups = (0, 1, 2) if group == 2 else (3,)
+        for which in range(2):
+            if side is other:
+                for g in groups:
+                    arrived(wbuf[which].at[0, pl.ds(0, 512 if g else 384), :], w_core.at[which, g])
+            off, cols = block_cols[which]
+            for s in range(SEQS):
+                at = pl.ds(s * ROWS, ROWS)
+                o = None if group == 2 else acc[which][side, at, :]
+                for g in groups:
+                    zq = lax.rem((zh, zh + ds, zh - ds, zh + 2)[g] + 4, 4)
+                    rows = pl.ds(pl.multiple_of(zq * 512, 512), 512)
+                    part_of = jnp.dot(mixed[at, rows], wbuf[which][side, rows, :], preferred_element_type=F32)
+                    o = part_of if o is None else o + part_of
+                if group == 2:
+                    acc[which][side, at, :] = o
+                else:
+                    out[s, :, pl.ds(pl.multiple_of(1024 * side + off, SIZE), cols)] = o.astype(BF16)
+
     keys(0, 0)
     keys(0, 1)
     theirs(0)
     ours(0)
     keys(1, 0)
-    keys(1, 1)
+    chip_sum(0)
     y_got_full(0, 0, 0, 0)
     y_got_full(0, 0, 1, 1)
+    keys(1, 1)
     outer_full(1, 4, 0)
-    chip_sum(0)
+    y_got_full(0, 0, 0, 1)
     theirs(1)
+    y_got_full(0, 0, 1, 0)
     ours(1)
-    questions(0, 0)
-    y_got_full(0, 0, 0, 1)
-    y_got_full(0, 0, 1, 0)
     outer_full(1, 4, 1)
-    questions(0, 1)
     chip_sum(1)
     questions(1, 0)
+    questions(0, 0)
+    y_got_full(1, 1, 1, 1)
     outer_full(0, 0, 0)
-    y_got_full(1, 1, 0, 0)
-    y_got_full(1, 1, 1, 1)
-    questions(1, 1)
+    y_got_full(1, 1, 1, 0)
     inner_full(1, 4, 0)
-    outer_full(0, 0, 1)
-    y_got_full(1, 1, 0, 1)
-    y_got_full(1, 1, 1, 0)
+    y_got_half(0, 0, 1)
+    x_sum(0)
     inner_full(1, 4, 1)
     y_got_half(0, 0, 0)
     outer_full(0, 1, 0)
-    y_got_half(0, 0, 1)
-    x_sum(0)
+    y_got_full(1, 2, 0, 1)
+    y_got_full(1, 1, 0, 1)
+    x_sum(1)
+    inner_full(0, 0, 0)
+    whole_sum(0)
+    outer_half(1, 4)
+    y_got_full(1, 3, 1, 0)
+    outer_full(0, 3, 0)
+    outer_full(0, 2, 0)
+    y_got_full(1, 3, 0, 0)
+    y_got_full(1, 3, 0, 1)
+    outer_full(0, 1, 1)
+    outer_full(0, 0, 1)
+    whole_sum(1)
+    outer_full(0, 3, 1)
+    questions(0, 1)
+    y_got_full(1, 2, 0, 0)
+    y_got_full(1, 2, 1, 1)
+    y_got_full(1, 2, 1, 0)
+    inner_full(0, 1, 0)
+    y_got_half(1, 1, 1)
+    inner_half(1, 4)
+    pass_on(0)
+    y_got_full(1, 4, 1, 0)
+    questions(1, 1)
     outer_full(0, 2, 1)
-    y_got_full(1, 2, 0, 0)
-    y_got_full(1, 2, 1, 0)
-    inner_full(0, 0, 0)
-    outer_full(0, 1, 1)
-    y_got_full(1, 2, 0, 1)
-    y_got_full(1, 2, 1, 1)
-    inner_full(0, 0, 1)
-    x_sum(1)
-    outer_full(0, 2, 0)
-    y_got_half(1, 1, 0)
-    y_got_half(1, 1, 1)
-    inner_full(0, 1, 0)
-    outer_half(1, 4)
-    y_got_full(1, 3, 0, 0)
-    y_got_full(1, 3, 1, 0)
-    whole_sum(0)
-    y_got_full(1, 3, 0, 1)
+    inner_full(0, 3, 0)
+    outer_half(0, 0)
+    y_got_half(1, 3, 0)
     y_got_full(1, 3, 1, 1)
-    outer_full(0, 3, 0)
-    inner_full(0, 2, 1)
-    outer_full(0, 3, 1)
+    y_got_full(1, 1, 0, 0)
+    answers(0, other)
+    inner_full(0, 2, 0)
+    pass_on(1)
+    outer_half(0, 1)
+    y_got_half(1, 2, 1)
     y_got_half(1, 2, 0)
-    y_got_half(1, 2, 1)
-    inner_full(0, 1, 1)
-    outer_half(0, 0)
-    y_got_full(1, 4, 0, 0)
-    y_got_full(1, 4, 1, 0)
-    whole_sum(1)
-    outer_half(0, 1)
-    y_got_half(1, 3, 0)
-    y_got_half(1, 3, 1)
-    inner_full(0, 2, 0)
-    pass_on(0)
-    answers(0, core)
-    inner_half(1, 4)
-    answers(0, other)
-    inner_full(0, 3, 0)
-    outer_half(0, 2)
-    inner_full(0, 3, 1)
-    pass_on(1)
-    answers(1, core)
     y_got_full(1, 4, 0, 1)
     y_got_full(1, 4, 1, 1)
+    outer_half(0, 3)
+    y_got_full(1, 4, 0, 0)
+    answers(1, other)
+    inner_full(0, 1, 1)
+    answers(1, core)
+    answers(0, core)
+    inner_full(0, 3, 1)
+    outer_half(0, 2)
+    y_got_half(1, 3, 1)
+    inner_full(0, 0, 1)
+    inner_full(0, 2, 1)
+    y_got_half(1, 1, 0)
+    project(2, core)
     inner_half(0, 0)
-    answers(1, other)
-    outer_half(0, 3)
-    inner_half(0, 1)
-    inner_half(0, 2)
+    project(2, other)
     y_got_half(1, 4, 0)
     y_got_half(1, 4, 1)
     inner_half(0, 3)
-
-    def project(n, s):
-        o = jnp.dot(mixed[pl.ds(s * ROWS, ROWS), :], wbuf[n], preferred_element_type=F32)
-        at = pl.ds(pl.multiple_of(512 * n, 512), 512)
-        out[s, :, at] = o.astype(BF16)
-
-    for i in range(2):
-        for s in range(SEQS):
-            project(2 * core + i, s)
-    arrived(wbuf.at[pl.ds(0, 2), pl.ds(0, 15 * SIZE), :], w_core)
-    for i in range(2):
-        for s in range(SEQS):
-            project(2 * other + i, s)
-
-    arrived(wbuf.at[:, pl.ds(0, 15 * SIZE), :], w_send)
+    inner_half(0, 2)
+    inner_half(0, 1)
+    project(3, core)
+    project(3, other)
+
+    for which in range(2):
+        arrived(wbuf[which].at[:, pl.ds(0, 15 * SIZE), :], w_send.at[which])
     for s in range(SEQS):
         arrived(send1.at[s], s_send.at[s, 0])
         for k in range(3):
@@ -420,14 +438,15 @@
                 vm((SEQS, 272, SIZE), BF16), vm((SEQS, 272, SIZE), BF16),
                 vm((SEQS, WIDTH, SIZE), BF16),
                 vm((SEQS * ROWS, WIDTH), BF16),
-                vm((4, WIDTH, 512), BF16),
+                vm((2, WIDTH, CUT), BF16), vm((2, WIDTH, 1024 - CUT), BF16),
+                vm((2, SEQS * ROWS, CUT), F32), vm((2, SEQS * ROWS, 1024 - CUT), F32),
                 dma((12,)),
                 dma((2, 2, 5, 2)), dma((2, 2, 5, 2)),
-                dma, dma, dma((SEQS, 9)),
+                dma((2,)), dma((2, 4)), dma((SEQS, 9)),
                 dma((SEQS,)), dma((SEQS, 3)), dma((SEQS,)), dma((SEQS, 3)), dma((SEQS,)),
             ],
             compiler_params=pltpu.CompilerParams(
-                collective_id=0, has_side_effects=True, vmem_limit_bytes=44 * 1024 * 1024
+                collective_id=0, has_side_effects=True, vmem_limit_bytes=48 * 1024 * 1024
             ),
         )(*(pltpu.with_memory_space_constraint(a, pltpu.HBM) for a in (asked_for, offered, contents, gate_rows, out_weight)))
 

time: 48 us -> 45.9 us (0.956)
  Pallas kernels: 46.6 us -> 44.5 us
    pallas_call x1, Pallas kernels: 46.6 us -> 44.5 us  [local(): pl.pallas_call(lambda *refs: kernel(count, *refs), out_shape=jax.ShapeDty...]
where the time goes in v3:
time: 45.9 us; the launch traced here: 45.8 us
  Pallas kernels  44.5 us (97%)
  local copies, waits for them, and re-layouts  1.32 us (3%)
    pallas_call x1, Pallas kernels, local(): pl.pallas_call(lambda *refs: kernel(count, *refs), out_shape=jax.ShapeDty...  44.5 us
    unnamed x1, local copies, waits for them, and re-layouts  1.32 us

profile of v3, /device:TPU:1, one launch (start us, length us, event | category | flops | bytes accessed | tf_op | source)
XLA Modules:
  0.0 45.8 jit_solution(9195695201559794648)
XLA Ops:
  0.0 44.5 %shard_map.55 = bf16[2,256,2048]{2,1,0:T(8,128)(2,1)S(1)} custom-call(bf16[2,256,16,128]{3,2,1,0:T(8,128)(2,1)} %refs_0_.1, bf16[2,256,16,128]{3,2,1,0:T(8,128)(2,1)} %refs_1_.1, bf16[2,256,16,128]{3,2,1,0:T(8,128)(2,1)} %refs_2_.1, bf16[2,256,16,128]{3,2,1,0:T(8,128)(2,1)} %refs_3_.1, bf16[128,2048]{1,0:T(8,128)(2,1)} %refs_4_.1), custom_call_target="tpu_custom_call" | custom-call | tf_op jit(solution)/shard_map/pallas_call | solution.py:423
  44.5 1.3 %copy.7 = bf16[2,256,2048]{2,1,0:T(8,128)(2,1)} copy(bf16[2,256,2048]{2,1,0:T(8,128)(2,1)S(1)} %shard_map.55) | data formatting | bytes 4194304

commit v4 on v3

--- a/solution.py
+++ b/solution.py
@@ -312,91 +312,91 @@
                     out[s, :, pl.ds(pl.multiple_of(1024 * side + off, SIZE), cols)] = o.astype(BF16)
 
     keys(0, 0)
+    questions(1, 0)
     keys(0, 1)
     theirs(0)
     ours(0)
     keys(1, 0)
     chip_sum(0)
     y_got_full(0, 0, 0, 0)
+    outer_full(1, 4, 0)
+    keys(1, 1)
+    theirs(1)
+    questions(0, 0)
+    y_got_full(0, 0, 0, 1)
     y_got_full(0, 0, 1, 1)
-    keys(1, 1)
-    outer_full(1, 4, 0)
-    y_got_full(0, 0, 0, 1)
-    theirs(1)
+    outer_full(1, 4, 1)
+    ours(1)
+    chip_sum(1)
+    outer_full(0, 0, 1)
+    outer_full(0, 0, 0)
+    inner_full(1, 4, 0)
+    x_sum(0)
     y_got_full(0, 0, 1, 0)
-    ours(1)
-    outer_full(1, 4, 1)
-    chip_sum(1)
-    questions(1, 0)
-    questions(0, 0)
-    y_got_full(1, 1, 1, 1)
-    outer_full(0, 0, 0)
-    y_got_full(1, 1, 1, 0)
-    inner_full(1, 4, 0)
-    y_got_half(0, 0, 1)
-    x_sum(0)
     inner_full(1, 4, 1)
     y_got_half(0, 0, 0)
     outer_full(0, 1, 0)
-    y_got_full(1, 2, 0, 1)
+    y_got_half(0, 0, 1)
     y_got_full(1, 1, 0, 1)
+    y_got_full(1, 1, 0, 0)
+    y_got_full(1, 1, 1, 1)
     x_sum(1)
-    inner_full(0, 0, 0)
+    outer_half(1, 4)
     whole_sum(0)
-    outer_half(1, 4)
+    y_got_full(1, 2, 1, 1)
+    questions(1, 1)
+    y_got_full(1, 2, 0, 0)
     y_got_full(1, 3, 1, 0)
-    outer_full(0, 3, 0)
-    outer_full(0, 2, 0)
-    y_got_full(1, 3, 0, 0)
-    y_got_full(1, 3, 0, 1)
-    outer_full(0, 1, 1)
-    outer_full(0, 0, 1)
-    whole_sum(1)
-    outer_full(0, 3, 1)
-    questions(0, 1)
-    y_got_full(1, 2, 0, 0)
-    y_got_full(1, 2, 1, 1)
     y_got_full(1, 2, 1, 0)
     inner_full(0, 1, 0)
+    questions(0, 1)
+    y_got_full(1, 2, 0, 1)
+    inner_full(0, 0, 0)
+    y_got_full(1, 3, 1, 1)
+    y_got_full(1, 3, 0, 0)
+    outer_full(0, 3, 0)
+    whole_sum(1)
+    outer_full(0, 2, 0)
+    y_got_full(1, 3, 0, 1)
+    outer_full(0, 3, 1)
+    outer_full(0, 2, 1)
+    outer_full(0, 1, 1)
+    inner_half(1, 4)
+    inner_full(0, 3, 0)
+    outer_half(0, 1)
+    pass_on(0)
+    outer_half(0, 0)
+    y_got_full(1, 4, 1, 0)
+    inner_full(0, 0, 1)
+    y_got_half(1, 1, 0)
+    inner_full(0, 2, 0)
+    answers(0, core)
+    inner_full(0, 3, 1)
+    y_got_full(1, 1, 1, 0)
+    answers(0, other)
+    inner_full(0, 2, 1)
+    pass_on(1)
+    answers(1, core)
     y_got_half(1, 1, 1)
-    inner_half(1, 4)
-    pass_on(0)
-    y_got_full(1, 4, 1, 0)
-    questions(1, 1)
-    outer_full(0, 2, 1)
-    inner_full(0, 3, 0)
-    outer_half(0, 0)
     y_got_half(1, 3, 0)
-    y_got_full(1, 3, 1, 1)
-    y_got_full(1, 1, 0, 0)
-    answers(0, other)
-    inner_full(0, 2, 0)
-    pass_on(1)
-    outer_half(0, 1)
     y_got_half(1, 2, 1)
-    y_got_half(1, 2, 0)
-    y_got_full(1, 4, 0, 1)
-    y_got_full(1, 4, 1, 1)
+    y_got_half(1, 3, 1)
     outer_half(0, 3)
     y_got_full(1, 4, 0, 0)
+    y_got_full(1, 4, 1, 1)
+    y_got_full(1, 4, 0, 1)
+    y_got_half(1, 2, 0)
+    inner_full(0, 1, 1)
     answers(1, other)
-    inner_full(0, 1, 1)
-    answers(1, core)
-    answers(0, core)
-    inner_full(0, 3, 1)
     outer_half(0, 2)
-    y_got_half(1, 3, 1)
-    inner_full(0, 0, 1)
-    inner_full(0, 2, 1)
-    y_got_half(1, 1, 0)
     project(2, core)
     inner_half(0, 0)
     project(2, other)
+    inner_half(0, 1)
+    inner_half(0, 3)
     y_got_half(1, 4, 0)
+    inner_half(0, 2)
     y_got_half(1, 4, 1)
-    inner_half(0, 3)
-    inner_half(0, 2)
-    inner_half(0, 1)
     project(3, core)
     project(3, other)
 

time: 45.9 us -> 43.5 us (0.948)
  Pallas kernels: 44.5 us -> 42.1 us
    pallas_call x1, Pallas kernels: 44.5 us -> 42.1 us  [local(): pl.pallas_call(lambda *refs: kernel(count, *refs), out_shape=jax.ShapeDty...]
where the time goes in v4:
time: 43.5 us
  Pallas kernels  42.1 us (97%)
  local copies, waits for them, and re-layouts  1.32 us (3%)
    pallas_call x1, Pallas kernels, local(): pl.pallas_call(lambda *refs: kernel(count, *refs), out_shape=jax.ShapeDty...  42.1 us
    unnamed x1, local copies, waits for them, and re-layouts  1.32 us

profile of v4, /device:TPU:1, one launch (start us, length us, event | category | flops | bytes accessed | tf_op | source)
XLA Modules:
  0.0 43.5 jit_solution(17213958352536008030)
XLA Ops:
  0.0 42.1 %shard_map.55 = bf16[2,256,2048]{2,1,0:T(8,128)(2,1)S(1)} custom-call(bf16[2,256,16,128]{3,2,1,0:T(8,128)(2,1)} %refs_0_.1, bf16[2,256,16,128]{3,2,1,0:T(8,128)(2,1)} %refs_1_.1, bf16[2,256,16,128]{3,2,1,0:T(8,128)(2,1)} %refs_2_.1, bf16[2,256,16,128]{3,2,1,0:T(8,128)(2,1)} %refs_3_.1, bf16[128,2048]{1,0:T(8,128)(2,1)} %refs_4_.1), custom_call_target="tpu_custom_call" | custom-call | tf_op jit(solution)/shard_map/pallas_call | solution.py:423
  42.2 1.3 %copy.7 = bf16[2,256,2048]{2,1,0:T(8,128)(2,1)} copy(bf16[2,256,2048]{2,1,0:T(8,128)(2,1)S(1)} %shard_map.55) | data formatting | bytes 4194304

commit v5 on v3

--- a/solution.py
+++ b/solution.py
@@ -317,86 +317,86 @@
     ours(0)
     keys(1, 0)
     chip_sum(0)
+    keys(1, 1)
+    theirs(1)
+    outer_full(1, 4, 0)
+    ours(1)
     y_got_full(0, 0, 0, 0)
+    questions(0, 0)
+    chip_sum(1)
     y_got_full(0, 0, 1, 1)
-    keys(1, 1)
-    outer_full(1, 4, 0)
+    outer_full(1, 4, 1)
+    y_got_full(1, 1, 0, 0)
     y_got_full(0, 0, 0, 1)
-    theirs(1)
+    outer_full(0, 0, 0)
+    questions(0, 1)
+    outer_full(0, 0, 1)
+    y_got_full(1, 1, 1, 1)
+    inner_full(1, 4, 0)
     y_got_full(0, 0, 1, 0)
-    ours(1)
-    outer_full(1, 4, 1)
-    chip_sum(1)
+    x_sum(0)
+    outer_full(0, 1, 0)
+    y_got_full(1, 1, 0, 1)
+    y_got_full(1, 2, 0, 0)
+    y_got_half(0, 0, 0)
     questions(1, 0)
-    questions(0, 0)
-    y_got_full(1, 1, 1, 1)
-    outer_full(0, 0, 0)
-    y_got_full(1, 1, 1, 0)
-    inner_full(1, 4, 0)
+    x_sum(1)
     y_got_half(0, 0, 1)
-    x_sum(0)
+    inner_full(0, 0, 1)
     inner_full(1, 4, 1)
-    y_got_half(0, 0, 0)
-    outer_full(0, 1, 0)
+    outer_half(1, 4)
+    whole_sum(0)
+    inner_full(0, 0, 0)
+    inner_full(0, 1, 0)
+    outer_full(0, 2, 0)
     y_got_full(1, 2, 0, 1)
-    y_got_full(1, 1, 0, 1)
-    x_sum(1)
-    inner_full(0, 0, 0)
-    whole_sum(0)
-    outer_half(1, 4)
     y_got_full(1, 3, 1, 0)
+    y_got_full(1, 2, 1, 1)
+    y_got_full(1, 2, 1, 0)
     outer_full(0, 3, 0)
-    outer_full(0, 2, 0)
+    outer_full(0, 2, 1)
+    whole_sum(1)
+    inner_half(1, 4)
+    y_got_half(1, 1, 1)
+    outer_full(0, 1, 1)
+    inner_full(0, 2, 0)
+    outer_full(0, 3, 1)
     y_got_full(1, 3, 0, 0)
     y_got_full(1, 3, 0, 1)
-    outer_full(0, 1, 1)
-    outer_full(0, 0, 1)
-    whole_sum(1)
-    outer_full(0, 3, 1)
-    questions(0, 1)
-    y_got_full(1, 2, 0, 0)
-    y_got_full(1, 2, 1, 1)
-    y_got_full(1, 2, 1, 0)
-    inner_full(0, 1, 0)
-    y_got_half(1, 1, 1)
-    inner_half(1, 4)
+    questions(1, 1)
+    outer_half(0, 0)
     pass_on(0)
+    outer_half(0, 1)
+    inner_full(0, 3, 0)
+    y_got_full(1, 3, 1, 1)
+    y_got_full(1, 4, 0, 0)
+    y_got_half(1, 2, 0)
+    y_got_half(1, 1, 0)
+    answers(0, other)
+    pass_on(1)
     y_got_full(1, 4, 1, 0)
-    questions(1, 1)
-    outer_full(0, 2, 1)
-    inner_full(0, 3, 0)
-    outer_half(0, 0)
-    y_got_half(1, 3, 0)
-    y_got_full(1, 3, 1, 1)
-    y_got_full(1, 1, 0, 0)
-    answers(0, other)
-    inner_full(0, 2, 0)
-    pass_on(1)
-    outer_half(0, 1)
-    y_got_half(1, 2, 1)
-    y_got_half(1, 2, 0)
     y_got_full(1, 4, 0, 1)
+    outer_half(0, 2)
     y_got_full(1, 4, 1, 1)
-    outer_half(0, 3)
-    y_got_full(1, 4, 0, 0)
-    answers(1, other)
+    answers(1, core)
     inner_full(0, 1, 1)
-    answers(1, core)
     answers(0, core)
     inner_full(0, 3, 1)
-    outer_half(0, 2)
+    inner_full(0, 2, 1)
+    answers(1, other)
+    inner_half(0, 0)
+    y_got_full(1, 1, 1, 0)
+    outer_half(0, 3)
+    y_got_half(1, 2, 1)
+    y_got_half(1, 3, 0)
     y_got_half(1, 3, 1)
-    inner_full(0, 0, 1)
-    inner_full(0, 2, 1)
-    y_got_half(1, 1, 0)
     project(2, core)
-    inner_half(0, 0)
+    inner_half(0, 2)
+    inner_half(0, 1)
     project(2, other)
     y_got_half(1, 4, 0)
     y_got_half(1, 4, 1)
     inner_half(0, 3)
-    inner_half(0, 2)
-    inner_half(0, 1)
     project(3, core)
     project(3, other)
 

time: 45.9 us -> 44 us (0.959)
  Pallas kernels: 44.5 us -> 42.6 us
    pallas_call x1, Pallas kernels: 44.5 us -> 42.6 us  [local(): pl.pallas_call(lambda *refs: kernel(count, *refs), out_shape=jax.ShapeDty...]
where the time goes in v5:
time: 44 us; the launch traced here: 43.9 us
  Pallas kernels  42.6 us (97%)
  local copies, waits for them, and re-layouts  1.32 us (3%)
    pallas_call x1, Pallas kernels, local(): pl.pallas_call(lambda *refs: kernel(count, *refs), out_shape=jax.ShapeDty...  42.6 us
    unnamed x1, local copies, waits for them, and re-layouts  1.32 us

profile of v5, /device:TPU:1, one launch (start us, length us, event | category | flops | bytes accessed | tf_op | source)
XLA Modules:
  0.0 43.9 jit_solution(11677020239756332815)
XLA Ops:
  0.0 42.6 %shard_map.55 = bf16[2,256,2048]{2,1,0:T(8,128)(2,1)S(1)} custom-call(bf16[2,256,16,128]{3,2,1,0:T(8,128)(2,1)} %refs_0_.1, bf16[2,256,16,128]{3,2,1,0:T(8,128)(2,1)} %refs_1_.1, bf16[2,256,16,128]{3,2,1,0:T(8,128)(2,1)} %refs_2_.1, bf16[2,256,16,128]{3,2,1,0:T(8,128)(2,1)} %refs_3_.1, bf16[128,2048]{1,0:T(8,128)(2,1)} %refs_4_.1), custom_call_target="tpu_custom_call" | custom-call | tf_op jit(solution)/shard_map/pallas_call | solution.py:423
  42.6 1.3 %copy.7 = bf16[2,256,2048]{2,1,0:T(8,128)(2,1)} copy(bf16[2,256,2048]{2,1,0:T(8,128)(2,1)S(1)} %shard_map.55) | data formatting | bytes 4194304
